TPU v7x, 32 devices: a whole 2x2x4 slice. The times are simulated.
32 devices in a mesh: row: 2 (over y), col: 4 (over z), depth: 4 (over x, core).
Axes of the slice: x: 2, y: 2, z: 4, core: 2. Of those that a mesh axis runs over, the one named last changes fastest.
Arguments:
- matrix: float32 [8, 2, 512, 8192], P(None, 'row', None, ('col', 'depth')), as said below
Outputs:
- factored: float32 [8, 2, 512, 8192], P(None, 'row', None, ('col', 'depth'))
Inputs may be any that keep to these rules, and one draw needn't show every extreme that they name: matrix is symmetric positive definite.
All inputs are finite; a program needn't handle non-finite values.
Results may differ from a plain program's by a relative error of at most 0.0001.
Values sent between devices are 32-bit elements; how exact they have to be, the bound alone decides.
A program may use at most 128 MiB of HBM per device.

v0:
```python
import jax
import jax.numpy as jnp
from jax import lax
from jax.sharding import PartitionSpec as P

PANELS = 2


def spread(x, axis, root):
    mine = lax.axis_index(axis) == root
    return lax.psum(jnp.where(mine, x, jnp.zeros_like(x)), axis)


def factor_blocks(lower_factor, blocks, block_ids, panel_index):
    count_rows, block_size, _ = blocks.shape
    solved = lax.linalg.triangular_solve(
        lower_factor,
        blocks.reshape(count_rows * block_size, block_size),
        left_side=False,
        lower=True,
        transpose_a=True,
    )
    solved = solved.reshape(count_rows, block_size, block_size)
    marks = block_ids[:, None, None]
    return jnp.where(
        marks > panel_index,
        solved,
        jnp.where(marks == panel_index, lower_factor[None], jnp.float32(0.0)),
    )


def body(matrix):
    blocks_here = matrix[:, 0, :, :]
    count_rows = blocks_here.shape[0]
    row_count = lax.axis_size("row")
    my_row = lax.axis_index("row")
    my_column = lax.axis_index(("col", "depth"))
    block_ids = jnp.arange(count_rows, dtype=jnp.int32) * row_count + my_row
    cross_slot = my_column // row_count
    cross_owner = my_column % row_count
    for panel_index in range(PANELS):
        diag_slot = panel_index // row_count
        diag_owner = panel_index % row_count
        raw_blocks = spread(blocks_here, ("col", "depth"), panel_index)
        diag_raw = spread(raw_blocks[diag_slot], "row", diag_owner)
        picked = lax.dynamic_index_in_dim(raw_blocks, cross_slot, 0, keepdims=False)
        cross_raw = spread(picked, "row", cross_owner)
        lower_factor = jnp.linalg.cholesky(diag_raw)
        panel_blocks = factor_blocks(lower_factor, raw_blocks, block_ids, panel_index)
        cross_block = lax.linalg.triangular_solve(
            lower_factor, cross_raw, left_side=False, lower=True, transpose_a=True
        )
        update = blocks_here - jnp.einsum(
            "axy,zy->axz", panel_blocks, cross_block, precision=lax.Precision.HIGHEST
        )
        trailing = jnp.where(block_ids[:, None, None] > panel_index, update, jnp.float32(0.0))
        blocks_here = jnp.where(
            my_column > panel_index,
            trailing,
            jnp.where(my_column == panel_index, panel_blocks, blocks_here),
        )
    return blocks_here[:, None, :, :]


def solution(mesh):
    placed = (P(None, "row", None, ("col", "depth")),)
    return jax.shard_map(
        body,
        mesh=mesh,
        in_specs=placed,
        out_specs=P(None, "row", None, ("col", "depth")),
        check_vma=False,
    )
```

profile of v0, /device:TPU:28, one launch (start us, length us, event | category | flops | bytes accessed | tf_op | source)
XLA Modules:
  0.0 962.0 jit_solution(8517915174789102627)
XLA Ops:
  23.8 170.0 %all-reduce.8.cloned.1.call-done = f32[8,512,512]{1,2,0:T(8,128)} async-done(((f32[8,512,512]{1,2,0:T(8,128)}), f32[8,512,512]{1,2,0:T(8,128)}) %all-reduce.8.cloned.1.call-update) | async-done | bytes 8388624 | tf_op jit(solution)/shard_map/psum | solution.py:11
  206.5 53.6 %all-reduce.14.cloned.1.call-done = (f32[512,512]{0,1:T(8,128)}, f32[512,512]{0,1:T(8,128)}) async-done(((f32[512,512]{0,1:T(8,128)}, f32[512,512]{0,1:T(8,128)}), (f32[512,512]{0,1:T(8,128)}, f32[512,512]{0,1:T(8,128)})) %all-reduce.14.cloned.1.call-update) | async-done | bytes 2097168 | tf_op jit(solution)/shard_map/psum | solution.py:11
  262.0 11.7 %cholesky.286 = f32[128,128]{1,0:T(8,128)S(1)} custom-call(f32[128,128]{1,0:T(8,128)S(1)} %cholesky.426), custom_call_target="Cholesky" | custom-call | tf_op jit(solution)/shard_map/jit(cholesky)/cholesky | solution.py:48
  273.8 9.8 %custom-call.31 = f32[1,128,128]{1,2,0:T(8,128)S(1)} custom-call(f32[1,128,128]{2,1,0:T(8,128)S(1)} %get-tuple-element.91), custom_call_target="InvertDiagBlocksLowerTriangular" | custom-call | tf_op jit(solution)/shard_map/jit(cholesky)/cholesky | solution.py:48
  284.3 11.7 %cholesky.305 = f32[128,128]{1,0:T(8,128)S(1)} custom-call(f32[128,128]{1,0:T(8,128)S(1)} %cholesky.430), custom_call_target="Cholesky" | custom-call | tf_op jit(solution)/shard_map/jit(cholesky)/cholesky | solution.py:48
  296.1 10.2 %custom-call.32 = f32[1,128,128]{1,2,0:T(8,128)S(1)} custom-call(f32[1,128,128]{2,1,0:T(8,128)S(1)} %get-tuple-element.88), custom_call_target="InvertDiagBlocksLowerTriangular" | custom-call | tf_op jit(solution)/shard_map/jit(cholesky)/cholesky | solution.py:48
  306.9 11.7 %cholesky.326 = f32[128,128]{1,0:T(8,128)S(1)} custom-call(f32[128,128]{1,0:T(8,128)S(1)} %cholesky.435), custom_call_target="Cholesky" | custom-call | tf_op jit(solution)/shard_map/jit(cholesky)/cholesky | solution.py:48
  319.3 9.8 %custom-call.33 = f32[1,128,128]{1,2,0:T(8,128)S(1)} custom-call(f32[1,128,128]{2,1,0:T(8,128)S(1)} %get-tuple-element.85), custom_call_target="InvertDiagBlocksLowerTriangular" | custom-call | tf_op jit(solution)/shard_map/jit(cholesky)/cholesky | solution.py:48
  329.7 11.7 %cholesky.343 = f32[128,128]{1,0:T(8,128)S(1)} custom-call(f32[128,128]{1,0:T(8,128)S(1)} %convolution_subtract_fusion.15), custom_call_target="Cholesky" | custom-call | tf_op jit(solution)/shard_map/jit(cholesky)/cholesky | solution.py:48
  354.0 39.3 %custom-call.34 = f32[4,128,128]{1,2,0:T(8,128)S(1)} custom-call(f32[4,128,128]{2,1,0:T(8,128)S(1)} %get-tuple-element.36), custom_call_target="InvertDiagBlocksLowerTriangular" | custom-call | tf_op jit(solution)/shard_map/triangular_solve/custom-call.3 | solution.py:16
  421.6 10.3 %fusion.19 = f32[4096,128]{1,0:T(8,128)S(1)} fusion(f32[4096,128]{0,1:T(8,128)S(1)} %fusion.112, f32[4096,128]{0,1:T(8,128)S(1)} %fusion.110, f32[4096,128]{0,1:T(8,128)S(1)} %bitcast.163, f32[4096,512]{1,0:T(8,128)S(1)} %bitcast.173, f32[512,512]{1,0:T(8,128)S(1)} %get-tuple-element.209), kind=kOutput, calls=%fused_computation.33 | convolution fusion | flops 2419589120 | bytes 10682368 | tf_op jit(solution)/shard_map/triangular_solve/dot.12 | solution.py:16
  456.7 32.3 %broadcast_select_fusion = (f32[8,512,512]{1,2,0:T(8,128)}, f32[8,512,512]{1,2,0:T(8,128)}) fusion(pred[]{:T(512)S(6)} %eq.41, f32[8,512,512]{1,2,0:T(8,128)} %copy.19, f32[512,512]{0,1:T(8,128)S(1)} %copy.18, pred[8]{0:T(512)(128)(4,1)S(1)} %get-tuple-element.98, pred[]{:T(512)S(6)} %eq.37, f32[512,128]{0,1:T(8,128)S(1)} %copy-done.2, ...), kind=kOutput, calls=%fused_computation.42 | convolution fusion | flops 12904562688 | bytes 35651604 | tf_op jit(solution)/shard_map/axy,zy->axz/dot_general | solution.py:53
  489.1 170.0 %all-reduce.10.cloned.1.call-done = f32[8,512,512]{1,2,0:T(8,128)} async-done(((f32[8,512,512]{1,2,0:T(8,128)}), f32[8,512,512]{1,2,0:T(8,128)}) %all-reduce.10.cloned.1.call-update) | async-done | bytes 8388624 | tf_op jit(solution)/shard_map/psum | solution.py:11
  671.9 53.4 %all-reduce.12.cloned.1.call-done = (f32[512,512]{0,1:T(8,128)}, f32[512,512]{0,1:T(8,128)}) async-done(((f32[512,512]{0,1:T(8,128)}, f32[512,512]{0,1:T(8,128)}), (f32[512,512]{0,1:T(8,128)}, f32[512,512]{0,1:T(8,128)})) %all-reduce.12.cloned.1.call-update) | async-done | bytes 2097168 | tf_op jit(solution)/shard_map/psum | solution.py:11
  727.2 11.7 %cholesky.358 = f32[128,128]{1,0:T(8,128)S(1)} custom-call(f32[128,128]{1,0:T(8,128)S(1)} %cholesky.439), custom_call_target="Cholesky" | custom-call | tf_op jit(solution)/shard_map/jit(cholesky)/cholesky | solution.py:48
  739.1 9.8 %custom-call.36 = f32[1,128,128]{1,2,0:T(8,128)S(1)} custom-call(f32[1,128,128]{2,1,0:T(8,128)S(1)} %get-tuple-element.81), custom_call_target="InvertDiagBlocksLowerTriangular" | custom-call | tf_op jit(solution)/shard_map/jit(cholesky)/cholesky | solution.py:48
  749.6 11.7 %cholesky.377 = f32[128,128]{1,0:T(8,128)S(1)} custom-call(f32[128,128]{1,0:T(8,128)S(1)} %cholesky.443), custom_call_target="Cholesky" | custom-call | tf_op jit(solution)/shard_map/jit(cholesky)/cholesky | solution.py:48
  762.7 9.9 %custom-call.37 = f32[1,128,128]{1,2,0:T(8,128)S(1)} custom-call(f32[1,128,128]{2,1,0:T(8,128)S(1)} %get-tuple-element.78), custom_call_target="InvertDiagBlocksLowerTriangular" | custom-call | tf_op jit(solution)/shard_map/jit(cholesky)/cholesky | solution.py:48
  773.3 11.7 %cholesky.398 = f32[128,128]{1,0:T(8,128)S(1)} custom-call(f32[128,128]{1,0:T(8,128)S(1)} %cholesky.448), custom_call_target="Cholesky" | custom-call | tf_op jit(solution)/shard_map/jit(cholesky)/cholesky | solution.py:48
  785.8 9.8 %custom-call.38 = f32[1,128,128]{1,2,0:T(8,128)S(1)} custom-call(f32[1,128,128]{2,1,0:T(8,128)S(1)} %get-tuple-element.75), custom_call_target="InvertDiagBlocksLowerTriangular" | custom-call | tf_op jit(solution)/shard_map/jit(cholesky)/cholesky | solution.py:48
  796.2 11.7 %cholesky.415 = f32[128,128]{1,0:T(8,128)S(1)} custom-call(f32[128,128]{1,0:T(8,128)S(1)} %convolution_subtract_fusion.14), custom_call_target="Cholesky" | custom-call | tf_op jit(solution)/shard_map/jit(cholesky)/cholesky | solution.py:48
  819.9 39.3 %custom-call.39 = f32[4,128,128]{1,2,0:T(8,128)S(1)} custom-call(f32[4,128,128]{2,1,0:T(8,128)S(1)} %get-tuple-element.38), custom_call_target="InvertDiagBlocksLowerTriangular" | custom-call | tf_op jit(solution)/shard_map/triangular_solve/custom-call.3 | solution.py:16
  887.3 10.3 %fusion.16 = f32[4096,128]{1,0:T(8,128)S(1)} fusion(f32[4096,128]{0,1:T(8,128)S(1)} %fusion.118, f32[4096,128]{0,1:T(8,128)S(1)} %fusion.116, f32[4096,128]{0,1:T(8,128)S(1)} %bitcast.166, f32[4096,512]{1,0:T(8,128)S(1)} %bitcast.179, f32[512,512]{1,0:T(8,128)S(1)} %get-tuple-element.208), kind=kOutput, calls=%fused_computation.32 | convolution fusion | flops 2419589120 | bytes 10682368 | tf_op jit(solution)/shard_map/triangular_solve/dot.12 | solution.py:16
  922.6 23.5 %select_bitcast_fusion = f32[8,1,512,512]{2,3,0,1:T(8,128)} fusion(f32[8,512,512]{1,2,0:T(8,128)} %get-tuple-element.95, f32[8,512,512]{1,2,0:T(8,128)} %copy.27, f32[512,512]{0,1:T(8,128)S(1)} %copy.26, pred[8]{0:T(512)(128)(4,1)S(1)} %get-tuple-element.100, pred[8]{0:T(512)(128)(4,1)S(1)} %get-tuple-element.101, pred[]{:T(512)S(6)} %eq.41, pred[]{:T(512)S(6)} %gt.24, ...), kind=kOutput, calls=%fused_computation.11 | convolution fusion | flops 12902465536 | bytes 27262994 | tf_op jit(solution)/shard_map/axy,zy->axz/dot_general | solution.py:53
  (140 shorter events, 203.9 us)
Async XLA Ops:
  6.5 187.3 %all-reduce.8.cloned.1.call-start = ((), (), s32[]{:S(2)}) async-start(), calls=%async_computation | async-start | bytes 16777216 | tf_op jit(solution)/shard_map/psum | solution.py:11
  23.8 236.3 %all-reduce.14.cloned.1.call-start = ((), (), s32[]{:S(2)}) async-start(), calls=%async_computation.3 | async-start | bytes 4194304 | tf_op jit(solution)/shard_map/psum | solution.py:11
  196.9 462.2 %all-reduce.10.cloned.1.call-start = ((), (), s32[]{:S(2)}) async-start(), calls=%async_computation.1 | async-start | bytes 16777216 | tf_op jit(solution)/shard_map/psum | solution.py:11
  260.0 1.7 copy-start
  399.9 12.2 %slice-start = ((s8[8388608]{0:T(1024)(128)(4,1)}), s8[4194304]{0:T(1024)(128)(4,1)S(1)}, s32[]{:S(2)}) async-start(s8[8388608]{0:T(1024)(128)(4,1)} %bitcast.170), calls=%async_computation.4 | async-start | bytes 8388608
  404.8 7.4 slice-start.1
  455.7 0.9 copy-start.2
  489.1 236.3 %all-reduce.12.cloned.1.call-start = ((), (), s32[]{:S(2)}) async-start(), calls=%async_computation.2 | async-start | bytes 4194304 | tf_op jit(solution)/shard_map/psum | solution.py:11
  725.3 1.7 copy-start.1
  865.8 12.2 %slice-start.2 = ((s8[8388608]{0:T(1024)(128)(4,1)}), s8[4194304]{0:T(1024)(128)(4,1)S(1)}, s32[]{:S(2)}) async-start(s8[8388608]{0:T(1024)(128)(4,1)} %bitcast.176), calls=%async_computation.6 | async-start | bytes 8388608
  870.7 7.4 slice-start.3
  921.6 0.9 copy-start.3
Sparse Core Ops, SparseCore 0:
  23.9 169.9 all-reduce.7
  197.0 62.9 all-reduce.13
  489.2 169.9 all-reduce.9
  662.3 62.9 all-reduce.11
where the time goes:
time: 969 us; the launch traced here: 962 us
  waiting for transfers between devices  447 us (46%)
  other arithmetic  260 us (27%)
  matrix products  140 us (14%)
  local copies, waits for them, and re-layouts  95.2 us (10%)
  between operations  19.1 us (2%)
    psum x4, waiting for transfers between devices, spread(): return lax.psum(jnp.where(mine, x, jnp.zeros_like(x)), axis)  447 us
    another operation x29, other arithmetic, body(): lower_factor = jnp.linalg.cholesky(diag_raw)  158 us
    another operation x7, other arithmetic, factor_blocks(): lax.linalg.triangular_solve(lower_factor, blocks.reshape(count_rows * blo...  87.3 us
    another operation x14, matrix products, factor_blocks(): lax.linalg.triangular_solve(lower_factor, blocks.reshape(count_rows * blo...  65.4 us
    dot_general x2, matrix products, body(): jnp.einsum('axy,zy->axz', panel_blocks, cross_block, precision=lax.Precis...  55.9 us
    another operation x29, local copies, waits for them, and re-layouts, factor_blocks(): lax.linalg.triangular_solve(lower_factor, blocks.reshape(count_rows * blo...  34.1 us
    psum x4, local copies, waits for them, and re-layouts, spread(): return lax.psum(jnp.where(mine, x, jnp.zeros_like(x)), axis)  22.5 us
  transfers between devices with their start and end apart: 4, of which 4 were waited for; matrix products, arithmetic and copies ran while one was open for 2% of the time, Pallas kernels for 0%

commit v1 on v0

v1 whole, which is shorter than its diff:
```python
import functools

import jax
import jax.numpy as jnp
from jax import lax
from jax.experimental import pallas as pl
from jax.experimental.pallas import tpu as pltpu
from jax.sharding import PartitionSpec as P

PANELS = 2
MESH = pl.DeviceIdType.MESH
HI = lax.Precision.HIGHEST
T = 128
NT = (((1,), (1,)), ((), ()))
TN = (((0,), (0,)), ((), ()))
NN = (((1,), (0,)), ((), ()))
DIAGS = ((0, 0), (0, 1), (1, 1))


def dot(a, b, dims=NN):
    return lax.dot_general(a, b, dims, precision=HI, preferred_element_type=jnp.float32)


def factor_tile(aug, tick):
    def strip(i, carry):
        j0 = pl.multiple_of(i * 8, 8)
        rows = aug[pl.ds(j0, 8), :]
        lane = lax.broadcasted_iota(jnp.int32, (8, T), 1)
        sub = lax.broadcasted_iota(jnp.int32, (8, T), 0)
        sub2 = lax.broadcasted_iota(jnp.int32, (8, 2 * T), 0)
        left = rows[:, :T]
        cols = [
            jnp.broadcast_to(
                jnp.sum(jnp.where(lane == j0 + t, left, 0.0), axis=1, keepdims=True), (8, T)
            )
            for t in range(8)
        ]
        for t in range(8):
            p = cols[t][t : t + 1, :]
            r = lax.rsqrt(p)
            r = r * (1.5 - 0.5 * p * r * r)
            coef = cols[t] * r
            for u in range(t + 1, 8):
                head = cols[u][t : t + 1, :] * r
                cols[u] = jnp.where(sub > t, cols[u] - coef * head, cols[u])
            wide_r = jnp.concatenate([r, r], axis=1)
            wide_c = jnp.concatenate([coef, coef], axis=1)
            head = rows[t : t + 1, :] * wide_r
            rows = jnp.where(sub2 == t, head, jnp.where(sub2 > t, rows - wide_c * head, rows))
        aug[pl.ds(j0, 8), :] = rows
        later = jnp.where(lane >= j0 + 8, rows[:, :T], 0.0)
        aug[...] -= dot(later, rows, TN)
        return carry

    lax.fori_loop(0, T // 8, strip, 0)


def gather_kernel(
    shape, first, m_ref, x0_ref, x1_ref, cross_ref, w_ref, u_ref,
    diag, work, aug, dsend, drecv, dloc, xsend, xrecv, xloc, csend, crecv, cloc,
):
    n_row, n_col, n_dep = shape
    slots, block, _ = m_ref.shape
    n_chunk = 2 * (slots - first)
    half = block // 2
    r = lax.axis_index("row")
    c = lax.axis_index("col")
    d = lax.axis_index("depth")
    across = lax.rem(d + n_dep // 2, n_dep)
    sib = d + 1 - 2 * lax.rem(d, 2)
    x_refs = (x0_ref, x1_ref)
    n_dc = block // T

    def dest(rr=None, cc=None, dd=None):
        return (r if rr is None else rr, c if cc is None else cc, d if dd is None else dd)

    def role(k):
        is_same = d == k
        is_xp = d == (k + n_dep // 2) % n_dep
        return is_same, is_xp

    def diag_copy(n, g, lane, to):
        part = diag.at[n, pl.ds(g * T, T), :]
        return pltpu.make_async_remote_copy(
            src_ref=part, dst_ref=part, send_sem=dsend.at[n, g, lane], recv_sem=drecv.at[n, g],
            device_id=to, device_id_type=MESH,
        )

    def diag_out(n):
        row, k = DIAGS[n]
        is_same, is_xp = role(k)
        root = is_same & (c == 0) & (r == row)
        out = [
            (is_same & (c < n_col - 1), dest(cc=lax.rem(c + 1, n_col))),
            (is_same, dest(dd=across)),
            (is_same | is_xp, dest(dd=sib)),
        ]
        for step in range(1, n_row):
            out.append((root, dest(rr=lax.rem(r + step, n_row))))
        return root, out

    def diag_load(n, g):
        return pltpu.make_async_copy(
            m_ref.at[0, pl.ds(g * T, T), :], diag.at[n, pl.ds(g * T, T), :], dloc.at[n, g]
        )

    def diag_step(n, g, wait):
        root, out = diag_out(n)

        @pl.when(root)
        def _():
            diag_load(n, g).wait()

        if wait:
            @pl.when(jnp.logical_not(root))
            def _():
                diag_copy(n, g, 0, dest(dd=sib)).wait_recv()

        order = out[3:] + out[:3]
        lanes = list(range(3, len(out))) + [0, 1, 2]
        for lane, (cond, to) in zip(lanes, order):
            @pl.when(cond)
            def _():
                diag_copy(n, g, lane, to).start()

    def diag_drain(n, g):
        _, out = diag_out(n)
        for lane, (cond, to) in enumerate(out):
            @pl.when(cond)
            def _():
                diag_copy(n, g, lane, to).wait_send()

    def x_part(ref, q, shift):
        return ref.at[q // 2 + shift, pl.ds(lax.rem(q, 2) * half, half), :]

    def x_copy(k, q, lane, to, root):
        dst = x_part(x_refs[k], q, 0)
        src = x_part(m_ref, q, first) if root else dst
        return pltpu.make_async_remote_copy(
            src_ref=src, dst_ref=dst, send_sem=xsend.at[k, q, lane], recv_sem=xrecv.at[k, q],
            device_id=to, device_id_type=MESH,
        )

    def x_local(k, q):
        return pltpu.make_async_copy(
            x_part(m_ref, q, first), x_part(x_refs[k], q, 0), xloc.at[k, q]
        )

    def x_out(k, q):
        is_same, is_xp = role(k)
        tree_a = lax.rem(q, 2) == 0
        tree_b = jnp.logical_not(tree_a)
        root = is_same & (c == 0)
        along = (c < n_col - 1) & ((is_same & tree_a) | (is_xp & tree_b))
        side = (
            (is_same & tree_a & (c >= 1))
            | (is_same & tree_b & (c == 0))
            | (is_xp & tree_b & (c >= 1))
        )
        back = is_xp & tree_a & (c == 1)
        return root, [
            (along, dest(cc=lax.rem(c + 1, n_col))),
            (side, dest(dd=across)),
            (is_same | is_xp, dest(dd=sib)),
            (back, dest(cc=jnp.zeros_like(c))),
        ]

    def x_send(k, q, as_root):
        root, out = x_out(k, q)
        for lane, (cond, to) in enumerate(out):
            @pl.when(cond & (root if as_root else jnp.logical_not(root)))
            def _():
                x_copy(k, q, lane, to, as_root).start()

    def x_tick(q):
        for k in range(PANELS):
            root, _ = x_out(k, q)

            @pl.when(jnp.logical_not(root))
            def _():
                x_copy(k, q, 0, dest(dd=sib), False).wait_recv()
                x_send(k, q, False)

    def x_drain(q):
        for k in range(PANELS):
            root, out = x_out(k, q)
            for lane, (cond, to) in enumerate(out):
                @pl.when(cond)
                def _():
                    x_copy(k, q, lane, to, False).wait_send()

            @pl.when(root)
            def _():
                x_local(k, q).wait()

    def cross_copy(k, step):
        return pltpu.make_async_remote_copy(
            src_ref=m_ref.at[0], dst_ref=cross_ref.at[k], send_sem=csend.at[k, step - 1],
            recv_sem=crecv.at[k], device_id=dest(rr=lax.rem(r + step, n_row)), device_id_type=MESH,
        )

    def cross_local(k):
        return pltpu.make_async_copy(m_ref.at[0], cross_ref.at[k], cloc.at[k])

    for n, (row, k) in enumerate(DIAGS):
        @pl.when((d == k) & (c == 0) & (r == row))
        def _():
            for g in range(n_dc):
                diag_load(n, g).start()
    for g in range(n_dc):
        diag_step(0, g, True)
    for n in (1, 2):
        root, _ = diag_out(n)

        @pl.when(root)
        def _():
            for g in range(n_dc):
                diag_step(n, g, False)

    def send_all(q, carry):
        for k in range(PANELS):
            x_send(k, q, True)
            root, _ = x_out(k, q)

            @pl.when(root)
            def _():
                x_local(k, q).start()
        return carry

    lax.fori_loop(0, n_chunk, send_all, 0)
    for k in range(PANELS):
        @pl.when(r == k)
        def _():
            cross_local(k).start()
            for step in range(1, n_row):
                cross_copy(k, step).start()

    def diag_late(n):
        root, _ = diag_out(n)

        @pl.when(jnp.logical_not(root))
        def _():
            for g in range(n_dc):
                diag_step(n, g, True)

    def eye(rows, columns, at):
        i = lax.broadcasted_iota(jnp.int32, (rows, columns), 0)
        j = lax.broadcasted_iota(jnp.int32, (rows, columns), 1)
        return jnp.where(i + at == j, jnp.float32(1.0), jnp.float32(0.0))

    per = -(-n_chunk // (PANELS * n_dc))

    def factor_block(panel):
        def tile(b, carry):
            at = pl.multiple_of(b * T, T)
            aug[:, :T] = work[pl.ds(at, T), pl.ds(at, T)]
            aug[:, T:] = eye(T, T, 0)
            factor_tile(aug, None)
            line = dot(aug[:, T:], work[pl.ds(at, T), :])
            work[pl.ds(at, T), :] = line
            lane = lax.broadcasted_iota(jnp.int32, (T, block), 1)
            aside = jnp.where(lane >= at + T, line[:, :block], 0.0)

            def tail(e, carry2):
                cols = pl.ds(pl.multiple_of(e * 2 * T, 2 * T), 2 * T)
                work[:, cols] -= dot(aside, work[pl.ds(at, T), cols], TN)
                return carry2

            lax.fori_loop(0, block // T, tail, 0)

            for e in range(per):
                q = (panel * n_dc + b) * per + e

                @pl.when(q < n_chunk)
                def _():
                    x_tick(jnp.minimum(q, n_chunk - 1))
            return carry

        lax.fori_loop(0, n_dc, tile, 0)

    def upper(x, at):
        i = lax.broadcasted_iota(jnp.int32, x.shape, 0)
        j = lax.broadcasted_iota(jnp.int32, x.shape, 1)
        return jnp.where(i + at <= j, x, 0.0)

    def lower(x, at):
        i = lax.broadcasted_iota(jnp.int32, x.shape, 0)
        j = lax.broadcasted_iota(jnp.int32, x.shape, 1)
        return jnp.where(i + at >= j, x, 0.0)

    def each_tile(f):
        def step(e, carry):
            f(pl.multiple_of(e * T, T))
            return carry

        lax.fori_loop(0, block // T, step, 0)

    def fill(n):
        def f(at):
            rows = pl.ds(at, T)
            work[rows, :block] = diag[n, rows, :]
            work[rows, block:] = eye(T, block, at)
        return f

    def keep(base):
        def f(at):
            rows = pl.ds(at, T)
            to = pl.ds(base + at, T)
            u_ref[to, base : base + block] = upper(work[rows, :block], at)
            w_ref[to, base : base + block] = lower(work[rows, block:], at)
        return f

    each_tile(fill(0))
    factor_block(0)
    each_tile(keep(0))
    diag_late(1)
    diag_late(2)

    def join(at):
        rows = pl.ds(at, T)
        u_ref[rows, block:] = dot(w_ref[rows, :block], diag[1])
        w_ref[rows, block:] = jnp.zeros((T, block), jnp.float32)
        u_ref[pl.ds(block + at, T), :block] = jnp.zeros((T, block), jnp.float32)

    each_tile(join)

    def second(at):
        rows = pl.ds(at, T)
        cols = pl.ds(block + at, T)
        top = u_ref[:block, block:]
        work[rows, :block] = diag[2, rows, :] - dot(u_ref[:block, cols], top, TN)
        work[rows, block:] = eye(T, block, at)

    each_tile(second)
    factor_block(1)
    each_tile(keep(block))

    def below(at):
        rows = pl.ds(at, T)
        cols = pl.ds(block + at, T)
        work[rows, :block] = dot(u_ref[:block, cols], w_ref[:block, :block], TN)

    each_tile(below)

    def corner(at):
        rows = pl.ds(block + at, T)
        w_ref[rows, :block] = -dot(w_ref[rows, block:], work[:, :block])

    each_tile(corner)

    for k in range(PANELS):
        @pl.when(r == k)
        def _():
            cross_local(k).wait()
            for step in range(1, n_row):
                cross_copy(k, step).wait_send()

        @pl.when(r != k)
        def _():
            cross_copy(k, 1).wait_recv()
    for n in range(len(DIAGS)):
        for g in range(n_dc):
            diag_drain(n, g)

    def drain(q, carry):
        x_drain(q)
        return carry

    lax.fori_loop(0, n_chunk, drain, 0)


def split(x):
    top = x.astype(jnp.bfloat16)
    return top, (x - top.astype(jnp.float32)).astype(jnp.bfloat16)


def update_kernel(first, keep_ref, m_ref, x0_ref, x1_ref, mat_ref, fix_ref, o_ref, top, low):
    s = pl.program_id(0)
    block = o_ref.shape[-1]

    @pl.when(s == 0)
    def _():
        for k in range(PANELS):
            a, b = split(mat_ref[k * block : (k + 1) * block, :])
            top[k] = a
            low[k] = b

    def go():
        base = jnp.where(keep_ref[0] > 0, m_ref[0], 0.0)
        acc = base
        for k, x_ref in enumerate((x0_ref, x1_ref)):
            a, b = split(x_ref[0])
            for left, right in ((a, top), (a, low), (b, top)):
                acc = acc - jnp.dot(left, right[k], preferred_element_type=jnp.float32)
        return acc

    if first:
        @pl.when(s == 0)
        def _():
            o_ref[0] = fix_ref[...]

        @pl.when(s > 0)
        def _():
            o_ref[0] = go()
    else:
        o_ref[0] = go()

        @pl.when((s == 0) & (keep_ref[1] > 0))
        def _():
            o_ref[0] = fix_ref[...]


def body(shape, matrix):
    n_row, n_col, n_dep = shape
    m = matrix.reshape(matrix.shape[0], matrix.shape[2], matrix.shape[3])
    slots, block, _ = m.shape
    order = PANELS * block
    first = 1 if n_row <= PANELS else 0
    n_chunk = 2 * (slots - first)
    n_dc = block // T
    f32 = jnp.float32
    dma = pltpu.SemaphoreType.DMA
    hbm = pl.BlockSpec(memory_space=pltpu.HBM)
    vmem = pl.BlockSpec(memory_space=pltpu.VMEM)
    panel = jax.ShapeDtypeStruct((slots - first, block, block), f32)
    x0, x1, cross, w, u = pl.pallas_call(
        functools.partial(gather_kernel, shape, first),
        out_shape=(
            panel, panel,
            jax.ShapeDtypeStruct((PANELS, block, block), f32),
            jax.ShapeDtypeStruct((order, order), f32),
            jax.ShapeDtypeStruct((order, order), f32),
        ),
        in_specs=[hbm],
        out_specs=(hbm, hbm, hbm, vmem, vmem),
        scratch_shapes=[
            pltpu.VMEM((len(DIAGS), block, block), f32),
            pltpu.VMEM((block, 2 * block), f32),
            pltpu.VMEM((T, 2 * T), f32),
            dma((len(DIAGS), n_dc, 2 + n_row)),
            dma((len(DIAGS), n_dc)),
            dma((len(DIAGS), n_dc)),
            dma((PANELS, n_chunk, 4)),
            dma((PANELS, n_chunk)),
            dma((PANELS, n_chunk)),
            dma((PANELS, n_row - 1)),
            dma((PANELS,)),
            dma((PANELS,)),
        ],
        compiler_params=pltpu.CompilerParams(has_side_effects=True, vmem_limit_bytes=48 << 20),
    )(m)

    j = lax.axis_index(("col", "depth"))
    r = lax.axis_index("row")
    own = cross.reshape(order, block)
    solved = jnp.dot(w, own, precision=HI)
    i1 = lax.broadcasted_iota(jnp.int32, (order, block), 0)
    i2 = lax.broadcasted_iota(jnp.int32, (order, block), 1)
    unit = jnp.where(i1 == i2 + j * block, f32(-1.0), f32(0.0))
    mat = lax.dot_general(w, jnp.where(j < PANELS, unit, solved), TN, precision=HI)
    rr = jnp.minimum(r, PANELS - 1)
    jj = jnp.minimum(j, PANELS - 1)
    fix = lax.dynamic_slice(u, (jj * block, rr * block), (block, block)).T
    fix = jnp.where(j < PANELS, fix, f32(0.0))
    flags = jnp.stack([j >= PANELS, r < PANELS]).astype(jnp.int32)

    one = (1, block, block)
    shifted = lambda s: (jnp.maximum(s - first, 0), 0, 0)
    out = pl.pallas_call(
        functools.partial(update_kernel, first),
        out_shape=jax.ShapeDtypeStruct(m.shape, f32),
        grid=(slots,),
        in_specs=[
            pl.BlockSpec(memory_space=pltpu.SMEM),
            pl.BlockSpec(one, lambda s: (s, 0, 0)),
            pl.BlockSpec(one, shifted),
            pl.BlockSpec(one, shifted),
            pl.BlockSpec((order, block), lambda s: (0, 0)),
            pl.BlockSpec((block, block), lambda s: (0, 0)),
        ],
        out_specs=pl.BlockSpec(one, lambda s: (s, 0, 0)),
        scratch_shapes=[
            pltpu.VMEM((PANELS, block, block), jnp.bfloat16),
            pltpu.VMEM((PANELS, block, block), jnp.bfloat16),
        ],
        compiler_params=pltpu.CompilerParams(vmem_limit_bytes=40 << 20),
    )(flags, m, x0, x1, mat, fix)
    return out.reshape(matrix.shape)


def solution(mesh):
    shape = (mesh.shape["row"], mesh.shape["col"], mesh.shape["depth"])
    placed = P(None, "row", None, ("col", "depth"))
    return jax.shard_map(
        functools.partial(body, shape),
        mesh=mesh,
        in_specs=(placed,),
        out_specs=placed,
        check_vma=False,
    )
```

time: 969 us -> 635 us (0.66)
  Pallas kernels: 0 us -> 609 us
  waiting for transfers between devices: 447 us -> 0 us
  other arithmetic: 260 us -> 1.39 us
  matrix products: 140 us -> 15.8 us
  local copies, waits for them, and re-layouts: 95.2 us -> 8.43 us
  between operations: 19.1 us -> 0.06 us
    pallas_call x0 -> x2, Pallas kernels: none -> 609 us  [the longest x1 593 us: body(): pl.pallas_call(functools.partial(gather_kernel, shape, first), out_shape=...]
    psum x4 -> x0, waiting for transfers between devices: 447 us -> none  [spread(): return lax.psum(jnp.where(mine, x, jnp.zeros_like(x)), axis)]
    another operation x36 -> x0, other arithmetic: 245 us -> none  [the longest x29 158 us: body(): lower_factor = jnp.linalg.cholesky(diag_raw)]
    another operation x40 -> x0, matrix products: 84.4 us -> none  [the longest x14 65.4 us: factor_blocks(): lax.linalg.triangular_solve(lower_factor, blocks.reshape(count_rows * blo...]
    dot_general x2, matrix products: 55.9 us -> 15.8 us  [the longest x1 8.96 us: body(): solved = jnp.dot(w, own, precision=HI)]
    another operation x37 -> x0, local copies, waits for them, and re-layouts: 34.4 us -> none  [the longest x29 34.1 us: factor_blocks(): lax.linalg.triangular_solve(lower_factor, blocks.reshape(count_rows * blo...]
    psum x4 -> x0, local copies, waits for them, and re-layouts: 22.5 us -> none  [spread(): return lax.psum(jnp.where(mine, x, jnp.zeros_like(x)), axis)]
    reshape x2 -> x0, local copies, waits for them, and re-layouts: 18.2 us -> none  [factor_blocks(): solved = solved.reshape(count_rows, block_size, block_size)]
  transfers between devices with their start and end apart: 4 -> 0, of which waited for: 4 -> 0; matrix products, arithmetic and copies ran while one was open for 2% -> 0% of each run, Pallas kernels for 0% -> 0%
where the time goes in v1:
time: 635 us
  Pallas kernels  609 us (96%)
  matrix products  15.8 us (2%)
  local copies, waits for them, and re-layouts  8.43 us (1%)
    pallas_call x1, Pallas kernels, body(): pl.pallas_call(functools.partial(gather_kernel, shape, first), out_shape=...  593 us
    pallas_call x1, Pallas kernels, body(): pl.pallas_call(functools.partial(update_kernel, first), out_shape=jax.Sha...  16.1 us

profile of v1, /device:TPU:28, one launch (start us, length us, event | category | flops | bytes accessed | tf_op | source)
XLA Modules:
  0.0 634.8 jit_solution(6877564938887347302)
XLA Ops:
  0.0 0.1 add_convert_fusion.keep_ref
  0.1 593.1 %shard_map.17 = (f32[7,512,512]{2,1,0:T(8,128)}, f32[7,512,512]{2,1,0:T(8,128)}, f32[2,512,512]{2,1,0:T(8,128)S(1)}, f32[1024,1024]{1,0:T(8,128)}, f32[1024,1024]{1,0:T(8,128)}) custom-call(f32[8,512,512]{2,1,0:T(8,128)} %bitcast.15), custom_call_target="tpu_custom_call" | custom-call | tf_op jit(solution)/shard_map/pallas_call | solution.py:426
  593.1 0.0 copy-start.1
  593.2 9.0 %fusion.12 = f32[1024,512]{1,0:T(8,128)S(1)} fusion(f32[1024,1024]{1,0:T(8,128)} %get-tuple-element.12, f32[1024,512]{1,0:T(8,128)S(1)} %bitcast.14), kind=kOutput, calls=%fused_computation.14 | convolution fusion | flops 6442450944 | bytes 8388608 | tf_op jit(solution)/shard_map/dot_general | solution.py:456
  602.1 0.0 copy-done.1
  602.1 6.8 %fusion.3.mat_ref = f32[1024,512]{1,0:T(8,128)S(1)} fusion(f32[1024,1024]{1,0:T(8,128)S(1)} %copy-done.1, f32[1024,512]{1,0:T(8,128)S(1)} %fusion.12, s32[512]{0:T(512)S(1)} %iota_add_fusion, pred[]{:T(512)S(6)} %lt.14), kind=kOutput, calls=%fused_computation.4 | convolution fusion | flops 6444023808 | bytes 8390657 | tf_op jit(solution)/shard_map/dot_general | solution.py:460
  609.0 5.3 copy.3
  614.3 1.3 select_bitcast_fusion.fix_ref
  615.6 0.0 copy-start
  615.6 3.1 copy-done
  618.7 16.1 %shard_map.18 = f32[8,512,512]{2,1,0:T(8,128)} custom-call(s32[2]{0:T(128)S(1)} %add_convert_fusion.keep_ref, f32[8,512,512]{2,1,0:T(8,128)} %bitcast.16, f32[7,512,512]{2,1,0:T(8,128)S(1)} %copy-done, f32[7,512,512]{2,1,0:T(8,128)} %get-tuple-element.11.x1_ref, f32[1024,512]{1,0:T(8,128)S(1)} %fusion.3.mat_ref, f32[512,512]{1,0:T(8,128)S(1)} %select_bitcast_fusion.fix_ref), custom_call_target="tpu_custom_call" | custom-call | tf_op jit(solution)/shard_map/pallas_call | solution.py:469
  (1 shorter events, 0.0 us)
Async XLA Ops:
  593.1 9.0 %copy-start.1 = (f32[1024,1024]{1,0:T(8,128)S(1)}, f32[1024,1024]{1,0:T(8,128)}, u32[]{:S(2)}) copy-start(f32[1024,1024]{1,0:T(8,128)} %get-tuple-element.12) | copy-start | bytes 12582916
  615.6 3.1 copy-start

commit v2 on v1

--- a/solution.py
+++ b/solution.py
@@ -50,6 +50,10 @@
         aug[pl.ds(j0, 8), :] = rows
         later = jnp.where(lane >= j0 + 8, rows[:, :T], 0.0)
         aug[...] -= dot(later, rows, TN)
+
+        @pl.when(lax.rem(i, 4) == 3)
+        def _():
+            tick(i // 4)
         return carry
 
     lax.fori_loop(0, T // 8, strip, 0)
@@ -78,6 +82,9 @@
         is_same = d == k
         is_xp = d == (k + n_dep // 2) % n_dep
         return is_same, is_xp
+
+    def hop_of(k):
+        return jnp.where(lax.rem(d, 2) == k % 2, 0, 1)
 
     def diag_copy(n, g, lane, to):
         part = diag.at[n, pl.ds(g * T, T), :]
@@ -172,14 +179,38 @@
             def _():
                 x_copy(k, q, lane, to, as_root).start()
 
-    def x_tick(q):
+    def tick(t):
+        for n in (1, 2):
+            row, k = DIAGS[n]
+            near = (d - lax.rem(d, 2)) == (k - k % 2)
+            hops = c + hop_of(k) + jnp.where(near, 0, 1) + jnp.where(r == row, 0, 1)
+            root, _ = diag_out(n)
+            e = t - hops
+            g = jnp.minimum(jnp.maximum(e, 0), n_dc - 1)
+
+            @pl.when(jnp.logical_not(root) & (e >= 0) & (e < n_dc))
+            def _():
+                diag_step(n, g, True)
         for k in range(PANELS):
-            root, _ = x_out(k, q)
-
-            @pl.when(jnp.logical_not(root))
-            def _():
-                x_copy(k, q, 0, dest(dd=sib), False).wait_recv()
-                x_send(k, q, False)
+            is_same, is_xp = role(k)
+            sib_hop = hop_of(k)
+            near = (d - lax.rem(d, 2)) == (k - k % 2)
+            for tree in range(2):
+                if tree == 0:
+                    far = jnp.where(c == 0, 3, c + 1)
+                    hops = jnp.where(near, c, far) + sib_hop
+                else:
+                    back = jnp.where(c == 0, 0, c + 2)
+                    hops = jnp.where(near, back, c + 1) + sib_hop
+                e = t - 2 * hops
+                q = jnp.minimum(jnp.maximum(e, 0), n_chunk - 1)
+                root = is_same & (c == 0)
+                now = (e >= 0) & (e < n_chunk) & (lax.rem(q, 2) == tree)
+
+                @pl.when(now & jnp.logical_not(root))
+                def _():
+                    x_copy(k, q, 0, dest(dd=sib), False).wait_recv()
+                    x_send(k, q, False)
 
     def x_drain(q):
         for k in range(PANELS):
@@ -235,27 +266,19 @@
             for step in range(1, n_row):
                 cross_copy(k, step).start()
 
-    def diag_late(n):
-        root, _ = diag_out(n)
-
-        @pl.when(jnp.logical_not(root))
-        def _():
-            for g in range(n_dc):
-                diag_step(n, g, True)
-
     def eye(rows, columns, at):
         i = lax.broadcasted_iota(jnp.int32, (rows, columns), 0)
         j = lax.broadcasted_iota(jnp.int32, (rows, columns), 1)
         return jnp.where(i + at == j, jnp.float32(1.0), jnp.float32(0.0))
 
-    per = -(-n_chunk // (PANELS * n_dc))
+    n_tick = T // 32
 
     def factor_block(panel):
         def tile(b, carry):
             at = pl.multiple_of(b * T, T)
             aug[:, :T] = work[pl.ds(at, T), pl.ds(at, T)]
             aug[:, T:] = eye(T, T, 0)
-            factor_tile(aug, None)
+            factor_tile(aug, lambda e: tick((panel * n_dc + b) * n_tick + e))
             line = dot(aug[:, T:], work[pl.ds(at, T), :])
             work[pl.ds(at, T), :] = line
             lane = lax.broadcasted_iota(jnp.int32, (T, block), 1)
@@ -267,13 +290,6 @@
                 return carry2
 
             lax.fori_loop(0, block // T, tail, 0)
-
-            for e in range(per):
-                q = (panel * n_dc + b) * per + e
-
-                @pl.when(q < n_chunk)
-                def _():
-                    x_tick(jnp.minimum(q, n_chunk - 1))
             return carry
 
         lax.fori_loop(0, n_dc, tile, 0)
@@ -313,8 +329,6 @@
     each_tile(fill(0))
     factor_block(0)
     each_tile(keep(0))
-    diag_late(1)
-    diag_late(2)
 
     def join(at):
         rows = pl.ds(at, T)
@@ -348,6 +362,11 @@
 
     each_tile(corner)
 
+    def rest(t, carry):
+        tick(t)
+        return carry
+
+    lax.fori_loop(PANELS * n_dc * n_tick, max(n_chunk + 2 * (n_col + 2), 32), rest, 0)
     for k in range(PANELS):
         @pl.when(r == k)
         def _():

time: 635 us -> 361 us (0.57)
  Pallas kernels: 609 us -> 335 us
    pallas_call x1, Pallas kernels: 593 us -> 319 us  [body(): pl.pallas_call(functools.partial(gather_kernel, shape, first), out_shape=...]
where the time goes in v2:
time: 361 us; the launch traced here: 360 us
  Pallas kernels  335 us (93%)
  matrix products  15.8 us (4%)
  local copies, waits for them, and re-layouts  8.43 us (2%)
    pallas_call x1, Pallas kernels, body(): pl.pallas_call(functools.partial(gather_kernel, shape, first), out_shape=...  319 us
    pallas_call x1, Pallas kernels, body(): pl.pallas_call(functools.partial(update_kernel, first), out_shape=jax.Sha...  16.1 us
    dot_general x1, matrix products, body(): solved = jnp.dot(w, own, precision=HI)  8.96 us

profile of v2, /device:TPU:28, one launch (start us, length us, event | category | flops | bytes accessed | tf_op | source)
XLA Modules:
  0.0 360.4 jit_solution(3327901141988235226)
XLA Ops:
  0.0 0.1 add_convert_fusion.keep_ref
  0.1 318.7 %shard_map.17 = (f32[7,512,512]{2,1,0:T(8,128)}, f32[7,512,512]{2,1,0:T(8,128)}, f32[2,512,512]{2,1,0:T(8,128)S(1)}, f32[1024,1024]{1,0:T(8,128)}, f32[1024,1024]{1,0:T(8,128)}) custom-call(f32[8,512,512]{2,1,0:T(8,128)} %bitcast.15), custom_call_target="tpu_custom_call" | custom-call | tf_op jit(solution)/shard_map/pallas_call | solution.py:445
  318.8 0.0 copy-start.1
  318.8 9.0 %fusion.12 = f32[1024,512]{1,0:T(8,128)S(1)} fusion(f32[1024,1024]{1,0:T(8,128)} %get-tuple-element.12, f32[1024,512]{1,0:T(8,128)S(1)} %bitcast.14), kind=kOutput, calls=%fused_computation.14 | convolution fusion | flops 6442450944 | bytes 8388608 | tf_op jit(solution)/shard_map/dot_general | solution.py:475
  327.7 0.0 copy-done.1
  327.7 6.8 %fusion.3.mat_ref = f32[1024,512]{1,0:T(8,128)S(1)} fusion(f32[1024,1024]{1,0:T(8,128)S(1)} %copy-done.1, f32[1024,512]{1,0:T(8,128)S(1)} %fusion.12, s32[512]{0:T(512)S(1)} %iota_add_fusion, pred[]{:T(512)S(6)} %lt.14), kind=kOutput, calls=%fused_computation.4 | convolution fusion | flops 6444023808 | bytes 8390657 | tf_op jit(solution)/shard_map/dot_general | solution.py:479
  334.6 5.3 %copy.3 = f32[1024,1024]{0,1:T(8,128)} copy(f32[1024,1024]{1,0:T(8,128)} %get-tuple-element.14) | data formatting | bytes 8388608 | tf_op jit(solution)/shard_map/pallas_call | solution.py:445
  339.9 1.3 select_bitcast_fusion.fix_ref
  341.2 0.0 copy-start
  341.3 3.1 copy-done
  344.3 16.1 %shard_map.18 = f32[8,512,512]{2,1,0:T(8,128)} custom-call(s32[2]{0:T(128)S(1)} %add_convert_fusion.keep_ref, f32[8,512,512]{2,1,0:T(8,128)} %bitcast.16, f32[7,512,512]{2,1,0:T(8,128)S(1)} %copy-done, f32[7,512,512]{2,1,0:T(8,128)} %get-tuple-element.11.x1_ref, f32[1024,512]{1,0:T(8,128)S(1)} %fusion.3.mat_ref, f32[512,512]{1,0:T(8,128)S(1)} %select_bitcast_fusion.fix_ref), custom_call_target="tpu_custom_call" | custom-call | tf_op jit(solution)/shard_map/pallas_call | solution.py:488
  (1 shorter events, 0.0 us)
Async XLA Ops:
  318.8 9.0 %copy-start.1 = (f32[1024,1024]{1,0:T(8,128)S(1)}, f32[1024,1024]{1,0:T(8,128)}, u32[]{:S(2)}) copy-start(f32[1024,1024]{1,0:T(8,128)} %get-tuple-element.12) | copy-start | bytes 12582916
  341.2 3.1 copy-start
